TPU v7x, 32 devices: a whole 2x2x4 slice. The times are simulated.
32 devices in a mesh: beam: 2 (over x), gx: 16 (over z, y, core).
Axes of the slice: x: 2, y: 2, z: 4, core: 2. Of those that a mesh axis runs over, the one named last changes fastest.
Arguments:
- filterbank: bfloat16 [4096, 2048], P(('beam', 'gx')), parts along dimension 0, may hold values from -61 to 61
- chan_delay: int32 [16, 2048], P(None, 'gx'), may hold values from 0 to 7
- sub_delay: int32 [1536, 64], replicated, may hold values from 0 to 15
- widths: int32 [1536], replicated, may hold values from 1 to 16
Outputs:
- snr: float32 [3072, 2048], P('beam', 'gx'), parts along dimension 0
There are 2 independent parts, one for each index of `beam`. A program takes and returns all parts, laid end to end along the dimension named above; an argument that names none is the same for every part. Nothing has to cross between parts.
All inputs are finite; a program needn't handle non-finite values.
Results may differ from a plain program's by a relative error of at most 0.00059.
Values may be sent and summed in bfloat16 or wider, within the bound.
No kernel may reach another device: no remote copies, remote signals or barrier semaphores. Data moves between devices by JAX's collectives and lax.ppermute only.
A program may use at most 128 MiB of HBM per device.

v0:
```python
import jax
import jax.numpy as jnp
from jax import lax
from jax.sharding import PartitionSpec as P

SUBCH = 32
DELAY_ONE = 8
DELAY_TWO = 16
WMAX = 16


def passed_along(block, axis, distance):
    devices = range(lax.axis_size(axis))
    route = [(i - distance, i) for i in devices if i - distance in devices]
    return lax.ppermute(block, axis, route)


def per_device(filterbank, chan_delay, sub_delay, widths):
    chan_count, samples = filterbank.shape
    groups = chan_delay.shape[0]
    device_count = lax.axis_size("gx")
    sub_count = chan_count // SUBCH
    slab_len = samples // device_count
    trials, band_count = sub_delay.shape
    per_group = trials // groups
    margin_len = DELAY_TWO + WMAX
    span_len = slab_len + WMAX
    padded = jnp.pad(filterbank, ((0, 0), (0, DELAY_ONE)))
    band_input = padded.reshape(sub_count, SUBCH, samples + DELAY_ONE)
    band_delays = jnp.transpose(chan_delay.reshape(groups, sub_count, SUBCH), (1, 0, 2))
    first_codes = jnp.arange(DELAY_ONE, dtype=jnp.int32)[None, :, None]

    def band_sum(inputs):
        band_rows, delay_rows = inputs
        stacked = jnp.stack(
            [band_rows[:, offset : offset + samples] for offset in range(DELAY_ONE)], 0
        )
        stacked = stacked.reshape(DELAY_ONE * SUBCH, samples)
        one_hot = (
            (delay_rows[:, None, :] == first_codes)
            .astype(jnp.bfloat16)
            .reshape(groups, DELAY_ONE * SUBCH)
        )
        return jnp.dot(one_hot, stacked, preferred_element_type=jnp.float32).astype(jnp.bfloat16)

    subbands = lax.map(band_sum, (band_input, band_delays))
    regrouped = lax.all_to_all(subbands, "gx", split_axis=2, concat_axis=0, tiled=True)
    following = passed_along(regrouped[:, :, :margin_len], "gx", -1)
    extended = jnp.concatenate([regrouped, following], 2)
    trial_delays = sub_delay.reshape(groups, per_group, band_count)
    second_codes = jnp.arange(DELAY_TWO, dtype=jnp.int32)[None, :, None]

    def group_series(inputs):
        group_index, delay_rows = inputs
        group_rows = lax.dynamic_index_in_dim(extended, group_index, 1, keepdims=False)
        stacked = jnp.stack(
            [group_rows[:, offset : offset + span_len] for offset in range(DELAY_TWO)], 0
        )
        stacked = stacked.reshape(DELAY_TWO * band_count, span_len)
        one_hot = (
            (delay_rows[:, None, :] == second_codes)
            .astype(jnp.bfloat16)
            .reshape(per_group, DELAY_TWO * band_count)
        )
        own_part = jnp.dot(one_hot, stacked[:, :slab_len], preferred_element_type=jnp.float32)
        tail_part = lax.dot_general(
            stacked[:, slab_len:],
            one_hot,
            (((0,), (1,)), ((), ())),
            preferred_element_type=jnp.float32,
        )
        return (own_part, tail_part)

    own_blocks, tail_blocks = lax.map(
        group_series, (jnp.arange(groups, dtype=jnp.int32), trial_delays)
    )
    own_series = own_blocks.reshape(trials, slab_len)
    tail_cols = jnp.transpose(tail_blocks, (0, 2, 1)).reshape(trials, WMAX)
    series = jnp.concatenate([own_series, tail_cols], 1)
    boxcar = jnp.zeros((trials, slab_len), jnp.float32)
    for offset in range(WMAX):
        boxcar = boxcar + jnp.where(
            offset < widths[:, None], series[:, offset : offset + slab_len], 0.0
        )
    totals, squares = lax.psum(
        (jnp.sum(own_series, axis=1), jnp.sum(own_series * own_series, axis=1)), "gx"
    )
    average = totals / samples
    variance = squares / samples - average * average
    width_float = widths.astype(jnp.float32)[:, None]
    return (boxcar - width_float * average[:, None]) / jnp.sqrt(
        width_float * (variance[:, None] + 1e-05)
    )


def solution(mesh):
    in_specs = (P(("beam", "gx"), None), P(None, "gx"), P(), P())
    out_specs = P("beam", "gx")
    return jax.shard_map(
        per_device, mesh=mesh, in_specs=in_specs, out_specs=out_specs, check_vma=False
    )
```

profile of v0, /device:TPU:0, one launch (start us, length us, event | category | flops | bytes accessed | tf_op | source)
XLA Modules:
  0.0 178.5 jit_solution(11185816409424602314)
XLA Ops:
  0.0 0.8 reshape.68
  0.8 1.1 pad.4
  1.9 4.6 %while.24 = (s32[]{:T(128)}, bf16[4,16,2048]{2,1,0:T(8,128)(2,1)S(1)}, s32[4,16,32]{2,0,1:T(4,128)S(1)}, bf16[4,32,2056]{2,1,0:T(8,128)(2,1)S(1)}, s32[]{:T(128)}) while((s32[]{:T(128)}, bf16[4,16,2048]{2,1,0:T(8,128)(2,1)S(1)}, s32[4,16,32]{2,0,1:T(4,128)S(1)}, bf16[4,32,2056]{2,1,0:T(8,128)(2,1)S(1)}, s32[]{:T(128)}) %tuple.66), condition=%wide.region_1.2_spmd.clone, body=%wide.region_0.1_spmd.clone.sunk | while | flops 16814080 | bytes 3486793 | solution.py:46
  2.7 0.3 fusion.95
  3.9 0.3 fusion.95
  5.0 0.3 fusion.95
  6.2 0.3 fusion.95
  6.5 1.4 copy.16
  7.8 2.1 %reshape.74 = bf16[16,2,4096]{2,1,0:T(2,128)(2,1)S(1)} reshape(bf16[2048,4,16]{2,1,0:T(4,128)(2,1)S(1)} %bitcast.225) | data formatting | bytes 524288
  10.0 17.2 %all_to_all.18 = bf16[16,2,4096]{2,1,0:T(2,128)(2,1)S(1)} all-to-all(bf16[16,2,4096]{2,1,0:T(2,128)(2,1)S(1)} %reshape.74), channel_id=1, replica_groups=mesh['beam'=2,'gx'=16] {'gx'}, dimensions={0} | all-to-all | bytes 524288 | tf_op jit(solution)/shard_map/all_to_all | solution.py:47
  27.2 1.4 reshape.75
  28.7 1.0 copy.17
  29.7 1.3 collective-permute-start
  31.2 1.9 %collective-permute-done = bf16[64,16,32]{2,0,1:T(8,128)(2,1)S(1)} collective-permute-done((bf16[64,16,32]{2,0,1:T(8,128)(2,1)S(1)}, bf16[64,16,32]{2,0,1:T(8,128)(2,1)S(1)}, u32[]{:S(2)}, u32[]{:S(2)}) %collective-permute-start) | collective-permute-done | bytes 65568 | tf_op jit(solution)/shard_map/ppermute | solution.py:15
  33.3 70.5 %while.25 = (s32[]{:T(128)}, f32[16,96,128]{2,1,0:T(8,128)S(1)}, f32[16,16,96]{2,1,0:T(8,128)S(1)}, s32[16,96,64]{1,0,2:T(8,128)S(1)}, s32[16]{0:T(128)S(1)}, /*...) while((s32[]{:T(128)}, f32[16,96,128]{2,1,0:T(8,128)S(1)}, ...), condition=%wide.region_3.4_spmd.clone, body=%wide.region_2.3_spmd.clone.sunk | while | flops 28409860 | bytes 2107547 | solution.py:74
  33.3 0.6 dynamic_slice.38
  37.1 0.3 fusion.100
  37.4 0.2 fusion.101
  37.7 0.6 dynamic_slice.38
  41.5 0.3 fusion.100
  41.9 0.2 fusion.101
  42.1 0.6 dynamic_slice.38
  45.9 0.3 fusion.100
  46.3 0.2 fusion.101
  46.5 0.6 dynamic_slice.38
  50.3 0.3 fusion.100
  50.7 0.2 fusion.101
  50.9 0.6 dynamic_slice.38
  54.7 0.3 fusion.100
  55.1 0.2 fusion.101
  55.3 0.6 dynamic_slice.38
  59.2 0.3 fusion.100
  59.5 0.2 fusion.101
  59.7 0.6 dynamic_slice.38
  63.6 0.3 fusion.100
  63.9 0.2 fusion.101
  64.1 0.6 dynamic_slice.38
  68.0 0.3 fusion.100
  68.3 0.2 fusion.101
  68.5 0.6 dynamic_slice.38
  72.4 0.3 fusion.100
  72.7 0.2 fusion.101
  72.9 0.6 dynamic_slice.38
  76.8 0.3 fusion.100
  77.1 0.2 fusion.101
  77.3 0.6 dynamic_slice.38
  81.2 0.3 fusion.100
  81.5 0.2 fusion.101
  81.7 0.6 dynamic_slice.38
  85.6 0.3 fusion.100
  85.9 0.2 fusion.101
  86.1 0.6 dynamic_slice.38
  90.0 0.3 fusion.100
  90.3 0.2 fusion.101
  90.5 0.6 dynamic_slice.38
  94.4 0.3 fusion.100
  94.9 0.6 dynamic_slice.38
  98.8 0.3 fusion.100
  99.4 0.6 dynamic_slice.38
  103.2 0.3 fusion.100
  103.8 0.6 fusion.66
  104.5 0.3 copy.19
  104.8 61.7 %all-reduce.1 = (f32[1536]{0:T(1024)S(1)}, f32[1536]{0:T(1024)S(1)}) all-reduce(f32[1536]{0:T(1024)S(1)} %reduce_sum.25, f32[1536]{0:T(1024)S(1)} %reduce_sum.23), channel_id=1, replica_groups=mesh['beam'=2,'gx'=16] {'gx'}, use_global_device_ids=true, to_apply=%region_7.8 | all-reduce | flops 3072 | bytes 24576 | tf_op jit(solution)/shard_map/psum | solution.py:85
  166.5 11.9 %fusion.25 = f32[1536,128]{1,0:T(8,128)} fusion(f32[1536,128]{1,0:T(8,128)S(1)} %bitcast.229, f32[1536,16]{1,0:T(8,128)S(1)} %bitcast.228, f32[1536]{0:T(1024)S(1)} %get-tuple-element.146, f32[1536]{0:T(1024)S(1)} %get-tuple-element.145, pred[1536]{0:T(1024)(128)(4,1)S(1)} %get-tuple-element.162, pred[1536]{0:T(1024)(128)(4,1)S(1)} %get-tuple-element.148, ...), kind=kLoop, calls=%fused_computation.100 | loop fusion | flops 9437184 | bytes 1708032 | tf_op jit(solution)/shard_map/div | solution.py:91
  (393 shorter events, 28.9 us)
Async XLA Ops:
  27.2 3.8 %copy-start.1 = (s32[1536]{0:T(1024)S(1)}, s32[1536]{0:T(1024)}, u32[]{:S(2)}) copy-start(s32[1536]{0:T(1024)} %param.11) | copy-start | bytes 18436
  27.2 3.8 %copy-start = (s32[1536,64]{0,1:T(8,128)S(1)}, s32[1536,64]{0,1:T(8,128)}, u32[]{:S(2)}) copy-start(s32[1536,64]{0,1:T(8,128)} %param.10) | copy-start | bytes 1179652
  29.7 3.4 %collective-permute-start = (bf16[64,16,32]{2,0,1:T(8,128)(2,1)S(1)}, bf16[64,16,32]{2,0,1:T(8,128)(2,1)S(1)}, u32[]{:S(2)}, u32[]{:S(2)}) collective-permute-start(bf16[64,16,32]{2,0,1:T(8,128)(2,1)S(1)} %bitcast.231), channel_id=1, source_target_pairs={{1,0},{2,1},{3,2},{4,3},{5,4},{6,5},{7,6},{8,7},{9,8},{10,9},{11,1... | collective-permute-start | bytes 196616 | tf_op jit(solution)/shard_map/ppermute | solution.py:15
where the time goes:
time: 179 us; the launch traced here: 178 us
  blocking collectives  78.9 us (44%)
  local copies, waits for them, and re-layouts  42.3 us (24%)
  loops' own time  28.1 us (16%)
  other arithmetic  16 us (9%)
  matrix products  9.84 us (5%)
  waiting for transfers between devices  1.88 us (1%)
    psum x1, blocking collectives, per_device(): lax.psum((jnp.sum(own_series, axis=1), jnp.sum(own_series * own_series, a...  61.7 us
    another operation x1, loops' own time, per_device(): lax.map(group_series, (jnp.arange(groups, dtype=jnp.int32), trial_delays))  27.8 us
    while x268, local copies, waits for them, and re-layouts  20.8 us
    all_to_all x1, blocking collectives, per_device(): lax.all_to_all(subbands, 'gx', split_axis=2, concat_axis=0, tiled=True)  17.2 us
    div x1, other arithmetic, per_device(): (boxcar - width_float * average[:, None]) / jnp.sqrt(width_float * (varia...  11.9 us
    dynamic_slice x32, local copies, waits for them, and re-layouts, per_device(): lax.map(group_series, (jnp.arange(groups, dtype=jnp.int32), trial_delays))  9.85 us
    dot_general x16, matrix products, group_series(): jnp.dot(one_hot, stacked[:, :slab_len], preferred_element_type=jnp.float32)  5 us
  transfers between devices with their start and end apart: 1, of which 1 were waited for; matrix products, arithmetic and copies ran while one was open for 0% of the time, Pallas kernels for 0%

commit v1 on v0

--- a/solution.py
+++ b/solution.py
@@ -7,6 +7,13 @@
 DELAY_ONE = 8
 DELAY_TWO = 16
 WMAX = 16
+
+
+def remake_entries(x0, dim_i, array_dim=0):
+    return jnp.concatenate(
+        lax.all_to_all(jnp.stack(jnp.split(x0, lax.axis_size("gx"), dim_i)), "gx", 0, 0),
+        axis=array_dim,
+    )
 
 
 def passed_along(block, axis, distance):
@@ -44,7 +51,7 @@
         return jnp.dot(one_hot, stacked, preferred_element_type=jnp.float32).astype(jnp.bfloat16)
 
     subbands = lax.map(band_sum, (band_input, band_delays))
-    regrouped = lax.all_to_all(subbands, "gx", split_axis=2, concat_axis=0, tiled=True)
+    regrouped = remake_entries(subbands, 2)
     following = passed_along(regrouped[:, :, :margin_len], "gx", -1)
     extended = jnp.concatenate([regrouped, following], 2)
     trial_delays = sub_delay.reshape(groups, per_group, band_count)

time: 179 us -> 174 us (0.972)
  local copies, waits for them, and re-layouts: 42.3 us -> 36.6 us
    unnamed x6 -> x19, local copies, waits for them, and re-layouts: 3.58 us -> 0.19 us
    while x269 -> x268, local copies, waits for them, and re-layouts: 22.2 us -> 20.8 us
where the time goes in v1:
time: 174 us; the launch traced here: 173 us
  blocking collectives  78.9 us (45%)
  local copies, waits for them, and re-layouts  36.6 us (21%)
  loops' own time  28.1 us (16%)
  other arithmetic  16 us (9%)
  matrix products  9.84 us (6%)
  waiting for transfers between devices  1.88 us (1%)
    psum x1, blocking collectives, per_device(): lax.psum((jnp.sum(own_series, axis=1), jnp.sum(own_series * own_series, a...  61.7 us
    another operation x1, loops' own time, per_device(): lax.map(group_series, (jnp.arange(groups, dtype=jnp.int32), trial_delays))  27.8 us
    while x268, local copies, waits for them, and re-layouts  20.8 us
    all_to_all x1, blocking collectives, remake_entries(): lax.all_to_all(jnp.stack(jnp.split(x0, lax.axis_size('gx'), dim_i)), 'gx'...  17.2 us
    div x1, other arithmetic, per_device(): (boxcar - width_float * average[:, None]) / jnp.sqrt(width_float * (varia...  11.9 us
    dynamic_slice x32, local copies, waits for them, and re-layouts, per_device(): lax.map(group_series, (jnp.arange(groups, dtype=jnp.int32), trial_delays))  9.85 us
    dot_general x16, matrix products, group_series(): jnp.dot(one_hot, stacked[:, :slab_len], preferred_element_type=jnp.float32)  5 us
    dot_general x16, matrix products, group_series(): lax.dot_general(stacked[:, slab_len:], one_hot, (((0,), (1,)), ((), ())),...  3.53 us
  transfers between devices with their start and end apart: 1, of which 1 were waited for; matrix products, arithmetic and copies ran while one was open for 0% of the time, Pallas kernels for 0%

profile of v1, /device:TPU:0, one launch (start us, length us, event | category | flops | bytes accessed | tf_op | source)
XLA Modules:
  0.0 172.9 jit_solution(4677755764921018603)
XLA Ops:
  0.0 0.8 reshape.71
  0.8 1.1 pad.4
  1.9 4.6 %while.24 = (s32[]{:T(128)}, bf16[4,16,2048]{2,1,0:T(8,128)(2,1)S(1)}, s32[4,16,32]{2,0,1:T(4,128)S(1)}, bf16[4,32,2056]{2,1,0:T(8,128)(2,1)S(1)}, s32[]{:T(128)}) while((s32[]{:T(128)}, bf16[4,16,2048]{2,1,0:T(8,128)(2,1)S(1)}, s32[4,16,32]{2,0,1:T(4,128)S(1)}, bf16[4,32,2056]{2,1,0:T(8,128)(2,1)S(1)}, s32[]{:T(128)}) %tuple.64), condition=%wide.region_1.2_spmd.clone, body=%wide.region_0.1_spmd.clone.sunk | while | flops 16814080 | bytes 3486793 | solution.py:53
  2.7 0.3 fusion.95
  3.9 0.3 fusion.95
  5.0 0.3 fusion.95
  6.2 0.3 fusion.95
  6.8 17.2 %all_to_all.5 = bf16[16,4,16,128]{3,2,1,0:T(8,128)(2,1)S(1)} all-to-all(bf16[16,4,16,128]{3,2,1,0:T(8,128)(2,1)S(1)} %constant_dynamic-update-slice_fusion.16), channel_id=1, replica_groups=mesh['beam'=2,'gx'=16] {'gx'}, dimensions={0} | all-to-all | bytes 524288 | tf_op jit(solution)/shard_map/all_to_all | solution.py:14
  24.1 1.3 collective-permute-start
  25.7 1.9 %collective-permute-done = bf16[64,16,32]{2,0,1:T(8,128)(2,1)S(1)} collective-permute-done((bf16[64,16,32]{2,0,1:T(8,128)(2,1)S(1)}, bf16[64,16,32]{2,0,1:T(8,128)(2,1)S(1)}, u32[]{:S(2)}, u32[]{:S(2)}) %collective-permute-start) | collective-permute-done | bytes 65568 | tf_op jit(solution)/shard_map/ppermute | solution.py:22
  27.7 70.5 %while.25 = (s32[]{:T(128)}, f32[16,96,128]{2,1,0:T(8,128)S(1)}, f32[16,16,96]{2,1,0:T(8,128)S(1)}, s32[16,96,64]{1,0,2:T(8,128)S(1)}, s32[16]{0:T(128)S(1)}, /*...) while((s32[]{:T(128)}, f32[16,96,128]{2,1,0:T(8,128)S(1)}, ...), condition=%wide.region_3.4_spmd.clone, body=%wide.region_2.3_spmd.clone.sunk | while | flops 28409860 | bytes 2107547 | solution.py:81
  27.7 0.6 dynamic_slice.38
  31.6 0.3 fusion.100
  31.9 0.2 fusion.101
  32.1 0.6 dynamic_slice.38
  36.0 0.3 fusion.100
  36.3 0.2 fusion.101
  36.5 0.6 dynamic_slice.38
  40.1 0.2 bitcast_compare_fusion.2
  40.4 0.3 fusion.100
  40.7 0.2 fusion.101
  40.9 0.6 dynamic_slice.38
  44.8 0.3 fusion.100
  45.1 0.2 fusion.101
  45.3 0.6 dynamic_slice.38
  49.2 0.3 fusion.100
  49.5 0.2 fusion.101
  49.7 0.6 dynamic_slice.38
  53.6 0.3 fusion.100
  53.9 0.2 fusion.101
  54.1 0.6 dynamic_slice.38
  58.0 0.3 fusion.100
  58.3 0.2 fusion.101
  58.5 0.6 dynamic_slice.38
  62.4 0.3 fusion.100
  62.7 0.2 fusion.101
  62.9 0.6 dynamic_slice.38
  66.8 0.3 fusion.100
  67.1 0.2 fusion.101
  67.3 0.6 dynamic_slice.38
  71.2 0.3 fusion.100
  71.5 0.2 fusion.101
  71.7 0.6 dynamic_slice.38
  75.6 0.3 fusion.100
  75.9 0.2 fusion.101
  76.2 0.6 dynamic_slice.38
  80.0 0.3 fusion.100
  80.3 0.2 fusion.101
  80.6 0.6 dynamic_slice.38
  84.4 0.3 fusion.100
  84.7 0.2 fusion.101
  85.0 0.6 dynamic_slice.38
  88.8 0.3 fusion.100
  89.1 0.2 fusion.101
  89.4 0.6 dynamic_slice.38
  93.2 0.3 fusion.100
  93.6 0.2 fusion.101
  93.8 0.6 dynamic_slice.38
  97.6 0.3 fusion.100
  98.0 0.2 fusion.101
  98.2 0.6 fusion.66
  99.0 0.3 copy.13
  99.2 61.7 %all-reduce.1 = (f32[1536]{0:T(1024)S(1)}, f32[1536]{0:T(1024)S(1)}) all-reduce(f32[1536]{0:T(1024)S(1)} %reduce_sum.25, f32[1536]{0:T(1024)S(1)} %reduce_sum.23), channel_id=1, replica_groups=mesh['beam'=2,'gx'=16] {'gx'}, use_global_device_ids=true, to_apply=%region_7.8 | all-reduce | flops 3072 | bytes 24576 | tf_op jit(solution)/shard_map/psum | solution.py:92
  160.9 11.9 %fusion.25 = f32[1536,128]{1,0:T(8,128)} fusion(f32[1536,128]{1,0:T(8,128)S(1)} %bitcast.254, f32[1536,16]{1,0:T(8,128)S(1)} %bitcast.253, f32[1536]{0:T(1024)S(1)} %get-tuple-element.136, f32[1536]{0:T(1024)S(1)} %get-tuple-element.135, pred[1536]{0:T(1024)(128)(4,1)S(1)} %get-tuple-element.152, pred[1536]{0:T(1024)(128)(4,1)S(1)} %get-tuple-element.138, ...), kind=kLoop, calls=%fused_computation.100 | loop fusion | flops 9437184 | bytes 1708032 | tf_op jit(solution)/shard_map/div | solution.py:98
  (406 shorter events, 28.4 us)
Async XLA Ops:
  6.5 18.9 %copy-start.1 = (s32[1536]{0:T(1024)S(1)}, s32[1536]{0:T(1024)}, u32[]{:S(2)}) copy-start(s32[1536]{0:T(1024)} %param.11) | copy-start | bytes 18436
  6.5 19.0 %copy-start = (s32[1536,64]{0,1:T(8,128)S(1)}, s32[1536,64]{0,1:T(8,128)}, u32[]{:S(2)}) copy-start(s32[1536,64]{0,1:T(8,128)} %param.10) | copy-start | bytes 1179652
  24.1 3.4 %collective-permute-start = (bf16[64,16,32]{2,0,1:T(8,128)(2,1)S(1)}, bf16[64,16,32]{2,0,1:T(8,128)(2,1)S(1)}, u32[]{:S(2)}, u32[]{:S(2)}) collective-permute-start(bf16[64,16,32]{2,0,1:T(8,128)(2,1)S(1)} %bitcast.256), channel_id=1, source_target_pairs={{1,0},{2,1},{3,2},{4,3},{5,4},{6,5},{7,6},{8,7},{9,8},{10,9},{11,1... | collective-permute-start | bytes 196616 | tf_op jit(solution)/shard_map/ppermute | solution.py:22
